TPU v7x, 256 devices: a whole 4x4x8 slice. The times are simulated.
256 devices in a mesh: seq: 16 (over z, core), head: 16 (over x, y).
Axes of the slice: x: 4, y: 4, z: 8, core: 2. Of those that a mesh axis runs over, the one named last changes fastest.
Arguments:
- grad_output: bfloat16 [16384, 4096], P('seq', 'head'), may hold values from -6 to 6
- out_weight: bfloat16 [4096, 8192], P('seq', 'head'), may hold values from -0.0625 to 0.0625
- ssd_out: bfloat16 [16384, 8192], P('seq', 'head'), may hold values from -520 to 520
- gate: bfloat16 [16384, 8192], P('seq', 'head'), may hold values from -5 to 5
- norm_weight: float32 [8192], P('head'), may hold values from 0.5 to 1.5
- time_step: float32 [128, 16384], P('head', 'seq'), may hold values from 0.01 to 0.1
- log_decay: float32 [128, 16384], P('head', 'seq'), may hold values from -0.7 to 0
- state_in: bfloat16 [16384, 8, 128], P('seq'), may hold values from -1.796875 to 1.796875
- state_out: bfloat16 [16384, 8, 128], P('seq'), may hold values from -1.796875 to 1.796875
- skip: float32 [128], P('head'), may hold values from 0.5 to 1.5
Outputs:
- grad_x: bfloat16 [16384, 8192], P('seq', 'head')
- grad_gate: bfloat16 [16384, 8192], P('seq', 'head')
- grad_out_weight: float32 [4096, 8192], P('seq', 'head')
All inputs are finite; a program needn't handle non-finite values.
Results may differ from a plain program's by a relative error of at most 0.014.
Values may be sent and summed in bfloat16 or wider, within the bound.
A program may use at most 128 MiB of HBM per device.

v0:
```python
import math
import jax
import jax.numpy as jnp
from jax import lax
from jax.sharding import Mesh
from jax.sharding import PartitionSpec as P

HEADS = 128
GROUPS = 8
BLOCK_LEN = 256
HEAD = ("head_0", "head_1")
SEQ = ("seq_0", "seq_1")
epsilon = 1e-05


def over_axes(x, axes):
    for axis in axes:
        x = lax.psum(x, axis)
    return x


def nothing_yet(x, identity):
    return jax.tree.map(
        lambda part, zero: jnp.zeros_like(part) + jnp.asarray(zero, part.dtype), x, identity
    )


def carried_in(x, axes, combine, identity):
    before = start = nothing_yet(x, identity)
    running = x
    for axis in reversed(axes):
        size, here = (lax.axis_size(axis), lax.axis_index(axis))
        pieces = jax.tree.map(lambda part: lax.all_gather(part, axis), running)
        inside, running = (start, start)
        for k in reversed(range(size)):
            passed = k > here
            running = combine(running, jax.tree.map(lambda part: part[k], pieces))
            inside = jax.tree.map(lambda new, old: jnp.where(passed, new, old), running, inside)
        before = combine(inside, before)
    return before


def on_device(
    grad_output,
    out_weight,
    ssd_out,
    gate,
    norm_weight,
    time_step,
    log_decay,
    state_in,
    state_out,
    skip,
):
    tok_rows = ssd_out.shape[0]
    local_width = ssd_out.shape[1]
    total_width = local_width * lax.axis_size(HEAD)
    full_grad = lax.all_gather(grad_output, HEAD, axis=1, tiled=True)
    values = ssd_out.astype(jnp.float32)
    gate_values = gate.astype(jnp.float32)
    sigmoid_gate = jax.nn.sigmoid(gate_values)
    silu_gate = gate_values * sigmoid_gate
    gated_values = values * silu_gate
    local_squares = jnp.sum(gated_values * gated_values, axis=1)
    columns = full_grad
    normed_grad = jnp.dot(
        columns,
        lax.all_gather(out_weight, SEQ, axis=0, tiled=True),
        preferred_element_type=jnp.float32,
    )
    squares = over_axes(local_squares, HEAD)
    weighted = over_axes(jnp.sum(norm_weight * normed_grad * gated_values, axis=1), HEAD)
    inverse_rms = lax.rsqrt(squares[:, None] / total_width + epsilon)
    normed = (gated_values * inverse_rms * norm_weight).astype(jnp.bfloat16)
    gated_grad = (
        inverse_rms * norm_weight * normed_grad
        - gated_values * inverse_rms**3 * weighted[:, None] / total_width
    )
    grad_gate = (
        gated_grad * values * sigmoid_gate * (1.0 + gate_values * (1.0 - sigmoid_gate))
    ).astype(jnp.bfloat16)
    grad_ssd = (gated_grad * silu_gate).astype(jnp.bfloat16)
    columns = full_grad
    weight_sum = lax.psum_scatter(
        lax.dot_general(
            columns, normed, (((0,), (0,)), ((), ())), preferred_element_type=jnp.float32
        ).astype(jnp.bfloat16),
        SEQ,
        scatter_dimension=0,
        tiled=True,
    ).astype(jnp.float32)
    grad_out_weight = weight_sum * (1.0 / math.sqrt(tok_rows * lax.axis_size(SEQ)))
    heads_here = time_step.shape[0]
    head_width = local_width // heads_here
    blocks = tok_rows // BLOCK_LEN
    state_width = state_in.shape[2]
    group_count = state_in.shape[1]
    first_head = lax.axis_index(HEAD) * heads_here
    head_ids = first_head + jnp.arange(heads_here, dtype=jnp.int32)
    group_ids = head_ids // (HEADS // GROUPS)
    group_pick = (group_ids[:, None] == jnp.arange(group_count, dtype=jnp.int32)[None, :]).astype(
        jnp.bfloat16
    )
    b_heads = jnp.einsum(
        "tgn,hg->htn", state_in, group_pick, preferred_element_type=jnp.float32
    ).astype(jnp.bfloat16)
    b_heads = b_heads.reshape(heads_here, blocks, BLOCK_LEN, state_width)
    c_heads = jnp.einsum(
        "tgn,hg->htn", state_out, group_pick, preferred_element_type=jnp.float32
    ).astype(jnp.bfloat16)
    c_heads = c_heads.reshape(heads_here, blocks, BLOCK_LEN, state_width)
    grad_heads = grad_ssd.reshape(tok_rows, heads_here, head_width).transpose(1, 0, 2)
    grad_heads = grad_heads.reshape(heads_here, blocks, BLOCK_LEN, head_width)
    cumulative = jnp.cumsum(log_decay.reshape(heads_here, blocks, BLOCK_LEN), axis=2)
    block_total = cumulative[..., -1]
    sequence_indices = jnp.arange(BLOCK_LEN)
    upper_mask = sequence_indices[None, :] >= sequence_indices[:, None]
    scores = jnp.einsum("hktn,hksn->hkts", b_heads, c_heads, preferred_element_type=jnp.float32)
    log_gap = cumulative[..., None, :] - cumulative[..., :, None]
    block_weights = jnp.where(upper_mask, scores * jnp.exp(jnp.minimum(log_gap, 0.0)), 0.0).astype(
        jnp.bfloat16
    )
    within = jnp.einsum(
        "hkts,hksp->hktp", block_weights, grad_heads, preferred_element_type=jnp.float32
    )
    grad_float = grad_heads.astype(jnp.float32)
    scaled = (jnp.exp(cumulative)[..., None] * grad_float).astype(jnp.bfloat16)
    block_state = jnp.einsum("hksp,hksn->hkpn", scaled, c_heads, preferred_element_type=jnp.float32)

    def fold_block(carried, inputs):
        state_now, total_now = inputs
        return (state_now + jnp.exp(total_now)[:, None, None] * carried, carried)

    zero_state = jnp.zeros((heads_here, head_width, state_width), jnp.float32)
    summary, inside = lax.scan(
        fold_block, zero_state, (block_state.transpose(1, 0, 2, 3), block_total.T), reverse=True
    )
    decay_total = jnp.exp(jnp.sum(block_total, axis=1))
    tail_decay = jnp.exp(
        jnp.sum(block_total, axis=1, keepdims=True) - jnp.cumsum(block_total, axis=1)
    )

    def combine_pair(earlier, later):
        return (later[0] * earlier[0], later[1] + later[0][:, None, None] * earlier[1])

    identity = (jnp.ones((heads_here,), jnp.float32), zero_state)
    prefix = carried_in((decay_total, summary), SEQ, combine_pair, identity)
    remote = prefix[1]
    full_states = inside.transpose(1, 0, 2, 3) + tail_decay[..., None, None] * remote[:, None]
    carry_low = full_states.astype(jnp.bfloat16)
    across = jnp.einsum("hkpn,hktn->hktp", carry_low, b_heads, preferred_element_type=jnp.float32)
    across = across * jnp.exp(block_total[..., None] - cumulative)[..., None]
    step_sizes = time_step.reshape(heads_here, blocks, BLOCK_LEN)
    grad_head = step_sizes[..., None] * (within + across) + skip[:, None, None, None] * grad_float
    grad_x = (
        grad_head.reshape(heads_here, tok_rows, head_width)
        .transpose(1, 0, 2)
        .reshape(tok_rows, local_width)
    )
    return (grad_x.astype(jnp.bfloat16), grad_gate, grad_out_weight)


def solution(mesh):
    finer = Mesh(mesh.devices.reshape(8, 2, 4, 4), ("seq_0", "seq_1", "head_0", "head_1"))
    return jax.shard_map(
        on_device,
        mesh=finer,
        in_specs=(
            P(SEQ, HEAD),
            P(SEQ, HEAD),
            P(SEQ, HEAD),
            P(SEQ, HEAD),
            P(HEAD),
            P(HEAD, SEQ),
            P(HEAD, SEQ),
            P(SEQ, None, None),
            P(SEQ, None, None),
            P(HEAD),
        ),
        out_specs=(P(SEQ, HEAD), P(SEQ, HEAD), P(SEQ, HEAD)),
        check_vma=False,
    )
```

profile of v0, /device:TPU:2, one launch (start us, length us, event | category | flops | bytes accessed | tf_op | source)
XLA Modules:
  0.0 294.2 jit_solution(11251501523468864543)
XLA Ops:
  8.7 1.3 dynamic-slice.1
  13.3 2.3 reduce-window.6
  16.2 1.5 copy.74
  17.7 2.6 copy.75
  20.4 2.4 all-reduce
  23.1 2.1 convolution_convert_fusion.1
  25.2 29.5 %all-gather.9.cloned.1.call-done = bf16[4096,512]{1,0:T(8,128)(2,1)} async-done(((bf16[256,512]{1,0:T(8,128)(2,1)}), bf16[4096,512]{1,0:T(8,128)(2,1)}) %all-gather.9.cloned.1.call-update) | async-done | bytes 4194320 | tf_op jit(solution)/shard_map/all_gather | solution.py:68
  54.7 82.9 %all-gather.7.cloned.1.call-done = bf16[1024,4096]{1,0:T(8,128)(2,1)} async-done(((bf16[1024,256]{1,0:T(8,128)(2,1)}), bf16[1024,4096]{1,0:T(8,128)(2,1)}) %all-gather.7.cloned.1.call-update) | async-done | bytes 8388624 | tf_op jit(solution)/shard_map/all_gather | solution.py:58
  137.6 11.3 %multiply_reduce_fusion.1 = (f32[1024]{0:T(1024)S(1)}, f32[1024]{0:T(1024)S(1)}, f32[1024,512]{0,1:T(8,128)}) fusion(bf16[1024,512]{0,1:T(8,128)(2,1)S(1)} %copy.74, bf16[1024,512]{0,1:T(8,128)(2,1)} %copy.75, f32[512]{0:T(512)S(1)} %copy-done.7, bf16[1024,4096]{1,0:T(8,128)(2,1)} %all-gather.7.cloned.1.call-done, ...), kind=kOutput, calls=%fused_computation.32 | convolution fusion | flops 4301256704 | bytes 16787456 | tf_op jit(solution)/shard_map/dot_general | solution.py:66
  148.8 8.7 %all-reduce.3 = (f32[1024]{0:T(1024)S(1)}, f32[1024]{0:T(1024)S(1)}) all-reduce(f32[1024]{0:T(1024)S(1)} %get-tuple-element.160, f32[1024]{0:T(1024)S(1)} %get-tuple-element.159), channel_id=1, replica_groups=mesh['seq_0'=8,'seq_1'=2,'head_0'=4,'head_1'=4] {'head_0'}, use_global_device_ids=true, to_apply=%region_6.0 | all-reduce | flops 2048 | bytes 16384 | tf_op jit(solution)/shard_map/psum | solution.py:18
  157.5 10.2 %all-reduce.2 = (f32[1024]{0:T(1024)S(1)}, f32[1024]{0:T(1024)S(1)}) all-reduce(f32[1024]{0:T(1024)S(1)} %get-tuple-element.175, f32[1024]{0:T(1024)S(1)} %get-tuple-element.176), channel_id=1, replica_groups=mesh['seq_0'=8,'seq_1'=2,'head_0'=4,'head_1'=4] {'head_1'}, use_global_device_ids=true, to_apply=%region_7.8 | all-reduce | flops 2048 | bytes 16384 | tf_op jit(solution)/shard_map/psum | solution.py:18
  167.8 4.7 %fusion.9 = (bf16[1024,512]{0,1:T(8,128)(2,1)}, bf16[1024,512]{0,1:T(8,128)(2,1)S(1)}) fusion(bf16[1024,512]{0,1:T(8,128)(2,1)S(1)} %copy.74, bf16[1024,512]{0,1:T(8,128)(2,1)} %copy.75, f32[1024]{0:T(1024)S(1)} %get-tuple-element.173, f32[1024]{0:T(1024)S(1)} %get-tuple-element.182, f32[1024,512]{0,1:T(8,128)} %get-tuple-element.195, f32[512]{0:T(512)S(1)} %copy-done.7, ...), kind=kLoop, calls=%fused_computation.20 | loop fusion | flops 11534336 | bytes 6305792 | tf_op jit(solution)/shard_map/convert_element_type | solution.py:81
  172.5 1.8 fusion.27
  174.3 4.5 %while.17 = (s32[]{:T(128)}, f32[8,64,128]{2,1,0:T(8,128)S(1)}, f32[4,8,64,128]{3,2,1,0:T(8,128)S(1)}, f32[4,8,64,128]{3,2,0,1:T(8,128)}, f32[4,8]{1,0:T(4,128)S(1)}, /*index=5*/s32[]{:T(128)}, s32[]{:T(128)}, s32[]{:T(128)}) while((s32[]{:T(128)}, f32[8,64,128]{2,1,0:T(8,128)S(1)}, f32[4,8,64,128]{3,2,1,0:T(8,128)S(1)}, ...), condition=%wide.region_9.10_spmd.clone, body=%wide.region_8.9_spmd.clone.sunk | while | flops 262148 | bytes 1310944 | solution.py:135
  179.8 2.2 all-gather
  183.0 11.0 %fusion.2 = bf16[4096,512]{0,1:T(8,128)(2,1)} fusion(bf16[1024,4096]{1,0:T(8,128)(2,1)} %all-gather.7.cloned.1.call-done, f32[512]{0:T(512)S(1)} %copy-done.7, bf16[1024,512]{0,1:T(8,128)(2,1)} %copy-done.2, f32[1024]{0:T(1024)S(1)} %get-tuple-element.181, bf16[1024,512]{0,1:T(8,128)(2,1)} %copy.75), kind=kOutput, calls=%fused_computation.7 | convolution fusion | flops 4302307328 | bytes 14686208 | tf_op jit(solution)/shard_map/dot_general | solution.py:85
  194.9 17.7 %all-reduce.1 = f32[64]{0:T(128)S(1)} all-reduce(f32[64]{0:T(128)S(1)} %copy-done.10), channel_id=4, replica_groups=mesh['seq_0'=8,'seq_1'=2,'head_0'=4,'head_1'=4] {'seq_0'}, use_global_device_ids=true, to_apply=%add.1 | all-reduce | flops 64 | bytes 512
  212.7 3.7 %convolution_convert_fusion.2 = bf16[8,1024,128]{2,0,1:T(8,128)(2,1)} fusion(bf16[1024,8,128]{2,1,0:T(8,128)(2,1)} %param.19, s32[8]{0:T(128)S(1)} %and_select_fusion), kind=kOutput, calls=%fused_computation.34 | convolution fusion | flops 17825856 | bytes 4194336 | tf_op jit(solution)/shard_map/tgn,hg->htn/dot_general | solution.py:104
  216.3 2.3 copy.86
  218.6 6.3 %fusion.3 = f32[8,4,256,64]{2,3,1,0:T(8,128)} fusion(f32[8,4,256]{2,1,0:T(4,128)S(1)} %copy.72, pred[256,256]{1,0:T(8,128)(4,1)S(1)} %iota_compare_fusion, bf16[8,4,256,128]{3,0,2,1:T(8,128)(2,1)} %bitcast.136, bf16[8,4,256,128]{3,0,2,1:T(8,128)(2,1)} %bitcast.130, bf16[8,8,4,8,256]{4,3,2,1,0:T(8,128)(2,1)} %bitcast.133), kind=kOutput, calls=%fused_computation.8 | convolution fusion | flops 815792128 | bytes 7438336 | tf_op jit(solution)/shard_map/hkts,hksp->hktp/dot_general | solution.py:123
  224.9 2.1 fusion.53
  227.2 3.3 %fusion.30 = bf16[8,4,8,8,256]{4,3,2,1,0:T(8,128)(2,1)S(1)} fusion(f32[8,4,256,64]{2,3,1,0:T(8,128)} %fusion.3, bf16[8,4,256,128]{3,0,2,1:T(8,128)(2,1)S(1)} %bitcast.131, f32[8]{0:T(128)S(1)} %copy-done.8, f32[8,4,256]{2,1,0:T(4,128)S(1)} %copy.83, f32[8,4,256]{2,1,0:T(4,128)S(1)} %copy.67, bf16[8,8,4,8,256]{4,3,2,1,0:T(8,128)(2,1)} %bitcast.134, ...), kind=kOutput, calls=%fused_computation.42 | convolution fusion | flops 138674176 | bytes 7667872 | tf_op jit(solution)/shard_map/hkpn,hktn->hktp/dot_general | solution.py:151
  230.6 1.3 copy.85
  231.9 53.7 %reduce-scatter.2.cloned.1.call-done = bf16[256,512]{0,1:T(8,128)(2,1)} async-done(((bf16[4096,512]{0,1:T(8,128)(2,1)}), bf16[256,512]{0,1:T(8,128)(2,1)}) %reduce-scatter.2.cloned.1.call-update) | async-done | bytes 262160 | tf_op jit(solution)/shard_map/reduce_scatter | solution.py:84
  (71 shorter events, 14.0 us)
Async XLA Ops:
  7.2 15.9 %copy-start = (bf16[1024,8,128]{2,1,0:T(8,128)(2,1)S(1)}, bf16[1024,8,128]{2,1,0:T(8,128)(2,1)}, u32[]{:S(2)}) copy-start(bf16[1024,8,128]{2,1,0:T(8,128)(2,1)} %param.20) | copy-start | bytes 6291460
  7.2 47.5 %all-gather.9.cloned.1.call-start = ((), (), s32[]{:S(2)}) async-start(), calls=%async_computation.2 | async-start | bytes 4456448 | tf_op jit(solution)/shard_map/all_gather | solution.py:68
  7.9 129.7 %all-gather.7.cloned.1.call-start = ((), (), s32[]{:S(2)}) async-start(), calls=%async_computation.1 | async-start | bytes 8912896 | tf_op jit(solution)/shard_map/all_gather | solution.py:58
  8.7 216.3 %all-gather.11.cloned.1.call-start = ((), (), s32[]{:S(2)}) async-start(), calls=%async_computation.3 | async-start | bytes 2359296 | tf_op jit(solution)/shard_map/all_gather | solution.py:33
  17.7 150.1 %copy-start.2 = (bf16[1024,512]{0,1:T(8,128)(2,1)}, bf16[1024,512]{0,1:T(8,128)(2,1)S(1)}, u32[]{:S(2)}) copy-start(bf16[1024,512]{0,1:T(8,128)(2,1)S(1)} %copy.74) | copy-start | bytes 3145732
  23.1 2.1 copy-start.9
  23.1 114.5 %copy-start.7 = (f32[512]{0:T(512)S(1)}, f32[512]{0:T(512)}, u32[]{:S(2)}) copy-start(f32[512]{0:T(512)} %param.16) | copy-start | bytes 6148
  167.8 4.7 %copy-start.5 = (bf16[8,1024,128]{2,0,1:T(8,128)(2,1)S(1)}, bf16[8,1024,128]{2,0,1:T(8,128)(2,1)}, u32[]{:S(2)}) copy-start(bf16[8,1024,128]{2,0,1:T(8,128)(2,1)} %convolution_convert_fusion.1) | copy-start | bytes 6291460
  172.5 1.8 copy-start.3
  178.8 1.0 copy-start.4
  182.8 102.8 %reduce-scatter.2.cloned.1.call-start = ((), (), s32[]{:S(2)}) async-start(), calls=%async_computation.4 | async-start | bytes 4456448 | tf_op jit(solution)/shard_map/reduce_scatter | solution.py:84
  194.0 0.8 copy-start.6
  194.1 0.8 copy-start.10
  224.9 2.1 copy-start.8
  224.9 2.2 copy-start.1
Sparse Core Ops, SparseCore 0:
  9.8 44.8 all-gather.8
  57.1 80.4 all-gather.6
  182.9 38.5 all-gather.10
  223.9 61.6 reduce-scatter.1
where the time goes:
time: 295 us; the launch traced here: 294 us
  waiting for transfers between devices  167 us (57%)
  blocking collectives  41.2 us (14%)
  matrix products  39.5 us (13%)
  other arithmetic  15.8 us (5%)
  between operations  15.3 us (5%)
  local copies, waits for them, and re-layouts  14.4 us (5%)
    all_gather x1, waiting for transfers between devices, on_device(): full_grad = lax.all_gather(grad_output, HEAD, axis=1, tiled=True)  82.9 us
    reduce_scatter x1, waiting for transfers between devices, on_device(): lax.psum_scatter(lax.dot_general(columns, normed, (((0,), (0,)), ((), ())...  53.7 us
    all_gather x1, waiting for transfers between devices, on_device(): lax.all_gather(out_weight, SEQ, axis=0, tiled=True)  29.5 us
    unnamed x2, blocking collectives  20.1 us
    psum x2, blocking collectives, over_axes(): x = lax.psum(x, axis)  18.9 us
    unnamed x32, local copies, waits for them, and re-layouts  13.2 us
    dot_general x1, matrix products, on_device(): jnp.dot(columns, lax.all_gather(out_weight, SEQ, axis=0, tiled=True), pre...  11.3 us
    dot_general x1, matrix products, on_device(): lax.dot_general(columns, normed, (((0,), (0,)), ((), ())), preferred_elem...  11 us
  transfers between devices with their start and end apart: 4, of which 3 were waited for; matrix products, arithmetic and copies ran while one was open for 15% of the time, Pallas kernels for 0%

commit v1 on v0

--- a/solution.py
+++ b/solution.py
@@ -55,7 +55,15 @@
     tok_rows = ssd_out.shape[0]
     local_width = ssd_out.shape[1]
     total_width = local_width * lax.axis_size(HEAD)
-    full_grad = lax.all_gather(grad_output, HEAD, axis=1, tiled=True)
+    full_grad = jnp.concatenate(
+        lax.all_to_all(
+            jnp.stack([grad_output for _ in range(lax.axis_size(HEAD))]),
+            axis_name=HEAD,
+            split_axis=0,
+            concat_axis=0,
+        ),
+        1,
+    )
     values = ssd_out.astype(jnp.float32)
     gate_values = gate.astype(jnp.float32)
     sigmoid_gate = jax.nn.sigmoid(gate_values)

time: 295 us -> 330 us (1.12)
  blocking collectives: 41.2 us -> 89 us
  waiting for transfers between devices: 167 us -> 143 us
  starting transfers between devices: 0.34 us -> 7.78 us
  local copies, waits for them, and re-layouts: 14.4 us -> 18.1 us
    all_to_all x0 -> x1, waiting for transfers between devices: none -> 89.6 us  [on_device(): lax.all_to_all(jnp.stack([grad_output for _ in range(lax.axis_size(HEAD))...]
    all_gather x1 -> x0, waiting for transfers between devices: 82.9 us -> none  [on_device(): full_grad = lax.all_gather(grad_output, HEAD, axis=1, tiled=True)]
    psum x2, blocking collectives: 18.9 us -> 64.4 us  [over_axes(): x = lax.psum(x, axis)]
    all_gather x1, waiting for transfers between devices: 29.5 us -> 0.01 us  [on_device(): lax.all_gather(out_weight, SEQ, axis=0, tiled=True)]
    all_to_all x0 -> x1, starting transfers between devices: none -> 7.48 us  [on_device(): lax.all_to_all(jnp.stack([grad_output for _ in range(lax.axis_size(HEAD))...]
    another operation x2 -> x3, local copies, waits for them, and re-layouts: 0.02 us -> 4.31 us  [the longest x1 4.29 us: on_device(): jnp.stack([grad_output for _ in range(lax.axis_size(HEAD))])]
    unnamed x32 -> x39, local copies, waits for them, and re-layouts: 13.2 us -> 13.3 us
  transfers between devices with their start and end apart: 4 -> 4, of which waited for: 3 -> 2; matrix products, arithmetic and copies ran while one was open for 15% -> 12% of each run, Pallas kernels for 0% -> 0%
where the time goes in v1:
time: 330 us; the launch traced here: 329 us
  waiting for transfers between devices  143 us (43%)
  blocking collectives  89 us (27%)
  matrix products  39.5 us (12%)
  local copies, waits for them, and re-layouts  18.1 us (5%)
  other arithmetic  15.8 us (5%)
  between operations  15.3 us (5%)
  starting transfers between devices  7.78 us (2%)
    all_to_all x1, waiting for transfers between devices, on_device(): lax.all_to_all(jnp.stack([grad_output for _ in range(lax.axis_size(HEAD))...  89.6 us
    psum x2, blocking collectives, over_axes(): x = lax.psum(x, axis)  64.4 us
    reduce_scatter x1, waiting for transfers between devices, on_device(): lax.psum_scatter(lax.dot_general(columns, normed, (((0,), (0,)), ((), ())...  53.1 us
    unnamed x2, blocking collectives  22.5 us
    unnamed x39, local copies, waits for them, and re-layouts  13.3 us
    dot_general x1, matrix products, on_device(): jnp.dot(columns, lax.all_gather(out_weight, SEQ, axis=0, tiled=True), pre...  11.3 us
    dot_general x1, matrix products, on_device(): lax.dot_general(columns, normed, (((0,), (0,)), ((), ())), preferred_elem...  11 us
    all_to_all x1, starting transfers between devices, on_device(): lax.all_to_all(jnp.stack([grad_output for _ in range(lax.axis_size(HEAD))...  7.48 us
  transfers between devices with their start and end apart: 4, of which 2 were waited for; matrix products, arithmetic and copies ran while one was open for 12% of the time, Pallas kernels for 0%

profile of v1, /device:TPU:2, one launch (start us, length us, event | category | flops | bytes accessed | tf_op | source)
XLA Modules:
  0.0 329.1 jit_solution(11686139407932693106)
XLA Ops:
  7.2 1.4 copy.78
  8.6 4.3 %stack.2 = bf16[16,1024,256]{1,2,0:T(8,128)(2,1)} broadcast(bf16[1024,256]{0,1:T(8,128)(2,1)S(1)} %copy.78), dimensions={1,2} | broadcast | bytes 8912896 | tf_op jit(solution)/shard_map/stack | solution.py:60
  12.9 7.5 %all-to-all-start = ((bf16[16,1024,256]{1,2,0:T(8,128)(2,1)}), bf16[16,1024,256]{1,2,0:T(8,128)(2,1)}, u32[]{:S(2)}, u32[]{:S(2)}) async-start(bf16[16,1024,256]{1,2,0:T(8,128)(2,1)} %stack.2), calls=%async_computation | async-start | bytes 16777216 | tf_op jit(solution)/shard_map/all_to_all | solution.py:59
  21.2 1.5 copy.76
  22.7 2.6 copy.77
  25.3 2.3 reduce-window.6
  30.8 2.4 all-reduce
  33.5 2.1 convolution_convert_fusion.1
  35.6 89.6 %all-to-all-done = bf16[16,1024,256]{1,2,0:T(8,128)(2,1)} async-done(((bf16[16,1024,256]{1,2,0:T(8,128)(2,1)}), bf16[16,1024,256]{1,2,0:T(8,128)(2,1)}, u32[]{:S(2)}, u32[]{:S(2)}) %all-to-all-start) | async-done | bytes 8388640 | tf_op jit(solution)/shard_map/all_to_all | solution.py:59
  125.2 11.3 %multiply_reduce_fusion.1 = (f32[1024]{0:T(1024)S(1)}, f32[1024]{0:T(1024)S(1)}, f32[1024,512]{0,1:T(8,128)}) fusion(bf16[1024,512]{0,1:T(8,128)(2,1)S(1)} %copy.76, bf16[1024,512]{0,1:T(8,128)(2,1)} %copy.77, f32[512]{0:T(512)S(1)} %copy-done.8, bf16[1024,4096]{0,1:T(8,128)(2,1)} %bitcast.6, bf16[4096,512]{1,0:T(8,128)(2,1)} %all-gather.6.cloned.1.call-done), kind=kOutput, calls=%fused_computation.32 | convolution fusion | flops 4301256704 | bytes 16787456 | tf_op jit(solution)/shard_map/dot_general | solution.py:74
  136.5 50.7 %all-reduce.3 = (f32[1024]{0:T(1024)S(1)}, f32[1024]{0:T(1024)S(1)}) all-reduce(f32[1024]{0:T(1024)S(1)} %get-tuple-element.160, f32[1024]{0:T(1024)S(1)} %get-tuple-element.159), channel_id=1, replica_groups=mesh['seq_0'=8,'seq_1'=2,'head_0'=4,'head_1'=4] {'head_0'}, use_global_device_ids=true, to_apply=%region_6.0 | all-reduce | flops 2048 | bytes 16384 | tf_op jit(solution)/shard_map/psum | solution.py:18
  187.2 13.7 %all-reduce.2 = (f32[1024]{0:T(1024)S(1)}, f32[1024]{0:T(1024)S(1)}) all-reduce(f32[1024]{0:T(1024)S(1)} %get-tuple-element.175, f32[1024]{0:T(1024)S(1)} %get-tuple-element.176), channel_id=1, replica_groups=mesh['seq_0'=8,'seq_1'=2,'head_0'=4,'head_1'=4] {'head_1'}, use_global_device_ids=true, to_apply=%region_7.8 | all-reduce | flops 2048 | bytes 16384 | tf_op jit(solution)/shard_map/psum | solution.py:18
  200.9 4.7 %fusion.9 = (bf16[1024,512]{0,1:T(8,128)(2,1)}, bf16[1024,512]{0,1:T(8,128)(2,1)S(1)}) fusion(bf16[1024,512]{0,1:T(8,128)(2,1)S(1)} %copy.76, bf16[1024,512]{0,1:T(8,128)(2,1)} %copy.77, f32[1024]{0:T(1024)S(1)} %get-tuple-element.173, f32[1024]{0:T(1024)S(1)} %get-tuple-element.182, f32[1024,512]{0,1:T(8,128)} %get-tuple-element.195, f32[512]{0:T(512)S(1)} %copy-done.8, ...), kind=kLoop, calls=%fused_computation.20 | loop fusion | flops 11534336 | bytes 6305792 | tf_op jit(solution)/shard_map/convert_element_type | solution.py:89
  205.6 1.8 fusion.27
  207.5 4.5 %while.17 = (s32[]{:T(128)}, f32[8,64,128]{2,1,0:T(8,128)S(1)}, f32[4,8,64,128]{3,2,1,0:T(8,128)S(1)}, f32[4,8,64,128]{3,2,0,1:T(8,128)}, f32[4,8]{1,0:T(4,128)S(1)}, /*index=5*/s32[]{:T(128)}, s32[]{:T(128)}, s32[]{:T(128)}) while((s32[]{:T(128)}, f32[8,64,128]{2,1,0:T(8,128)S(1)}, f32[4,8,64,128]{3,2,1,0:T(8,128)S(1)}, ...), condition=%wide.region_9.10_spmd.clone, body=%wide.region_8.9_spmd.clone.sunk | while | flops 262148 | bytes 1310936 | solution.py:143
  213.0 2.2 all-gather
  216.2 11.0 %fusion.2 = bf16[4096,512]{0,1:T(8,128)(2,1)} fusion(bf16[1024,4096]{0,1:T(8,128)(2,1)} %bitcast.6, f32[512]{0:T(512)S(1)} %copy-done.8, bf16[1024,512]{0,1:T(8,128)(2,1)} %copy-done.2, f32[1024]{0:T(1024)S(1)} %get-tuple-element.181, bf16[1024,512]{0,1:T(8,128)(2,1)} %copy.77), kind=kOutput, calls=%fused_computation.7 | convolution fusion | flops 4302307328 | bytes 14686208 | tf_op jit(solution)/shard_map/dot_general | solution.py:93
  228.0 20.0 %all-reduce.1 = f32[64]{0:T(128)S(1)} all-reduce(f32[64]{0:T(128)S(1)} %copy-done.11), channel_id=4, replica_groups=mesh['seq_0'=8,'seq_1'=2,'head_0'=4,'head_1'=4] {'seq_0'}, use_global_device_ids=true, to_apply=%add.1 | all-reduce | flops 64 | bytes 512
  248.1 3.7 %convolution_convert_fusion.2 = bf16[8,1024,128]{2,0,1:T(8,128)(2,1)} fusion(bf16[1024,8,128]{2,1,0:T(8,128)(2,1)} %param.19, s32[8]{0:T(128)S(1)} %and_select_fusion), kind=kOutput, calls=%fused_computation.34 | convolution fusion | flops 17825856 | bytes 4194336 | tf_op jit(solution)/shard_map/tgn,hg->htn/dot_general | solution.py:112
  251.9 2.3 copy.89
  254.2 6.3 %fusion.3 = f32[8,4,256,64]{2,3,1,0:T(8,128)} fusion(f32[8,4,256]{2,1,0:T(4,128)S(1)} %copy.74, pred[256,256]{1,0:T(8,128)(4,1)S(1)} %iota_compare_fusion, bf16[8,4,256,128]{3,0,2,1:T(8,128)(2,1)} %bitcast.139, bf16[8,4,256,128]{3,0,2,1:T(8,128)(2,1)} %bitcast.133, bf16[8,8,4,8,256]{4,3,2,1,0:T(8,128)(2,1)} %bitcast.136), kind=kOutput, calls=%fused_computation.8 | convolution fusion | flops 815792128 | bytes 7438336 | tf_op jit(solution)/shard_map/hkts,hksp->hktp/dot_general | solution.py:131
  260.4 2.1 fusion.53
  262.7 3.3 %fusion.30 = bf16[8,4,8,8,256]{4,3,2,1,0:T(8,128)(2,1)S(1)} fusion(f32[8,4,256,64]{2,3,1,0:T(8,128)} %fusion.3, bf16[8,4,256,128]{3,0,2,1:T(8,128)(2,1)S(1)} %bitcast.134, f32[8]{0:T(128)S(1)} %copy-done.9, f32[8,4,256]{2,1,0:T(4,128)S(1)} %copy.86, f32[8,4,256]{2,1,0:T(4,128)S(1)} %copy.69, bf16[8,8,4,8,256]{4,3,2,1,0:T(8,128)(2,1)} %bitcast.137, ...), kind=kOutput, calls=%fused_computation.42 | convolution fusion | flops 138674176 | bytes 7667872 | tf_op jit(solution)/shard_map/hkpn,hktn->hktp/dot_general | solution.py:159
  267.4 53.1 %reduce-scatter.2.cloned.1.call-done = bf16[256,512]{0,1:T(8,128)(2,1)} async-done(((bf16[4096,512]{0,1:T(8,128)(2,1)}), bf16[256,512]{0,1:T(8,128)(2,1)}) %reduce-scatter.2.cloned.1.call-update) | async-done | bytes 262160 | tf_op jit(solution)/shard_map/reduce_scatter | solution.py:92
  (78 shorter events, 13.8 us)
Async XLA Ops:
  7.2 26.3 %copy-start = (bf16[1024,8,128]{2,1,0:T(8,128)(2,1)S(1)}, bf16[1024,8,128]{2,1,0:T(8,128)(2,1)}, u32[]{:S(2)}) copy-start(bf16[1024,8,128]{2,1,0:T(8,128)(2,1)} %param.20) | copy-start | bytes 6291460
  12.9 112.3 %all-to-all-start = ((bf16[16,1024,256]{1,2,0:T(8,128)(2,1)}), bf16[16,1024,256]{1,2,0:T(8,128)(2,1)}, u32[]{:S(2)}, u32[]{:S(2)}) async-start(bf16[16,1024,256]{1,2,0:T(8,128)(2,1)} %stack.2), calls=%async_computation | async-start | bytes 16777216 | tf_op jit(solution)/shard_map/all_to_all | solution.py:59
  20.3 104.8 %all-gather.6.cloned.1.call-start = ((), (), s32[]{:S(2)}) async-start(), calls=%async_computation.2 | async-start | bytes 4456448 | tf_op jit(solution)/shard_map/all_gather | solution.py:76
  21.1 239.3 %all-gather.8.cloned.1.call-start = ((), (), s32[]{:S(2)}) async-start(), calls=%async_computation.3 | async-start | bytes 2359296 | tf_op jit(solution)/shard_map/all_gather | solution.py:33
  21.1 4.2 %copy-start.6 = (f32[8,1024]{1,0:T(8,128)S(1)}, f32[8,1024]{1,0:T(8,128)}, u32[]{:S(2)}) copy-start(f32[8,1024]{1,0:T(8,128)} %param.18) | copy-start | bytes 98308
  21.2 7.1 %copy-start.13 = (u32[256]{0:T(256)S(1)}, u32[256]{0:T(256)}, u32[]{:S(2)}) copy-start(u32[256]{0:T(256)} %constant.117) | copy-start | bytes 3076
  21.2 7.7 %copy-start.12 = (u32[256]{0:T(256)S(1)}, u32[256]{0:T(256)}, u32[]{:S(2)}) copy-start(u32[256]{0:T(256)} %constant.122) | copy-start | bytes 3076
  22.7 178.2 %copy-start.2 = (bf16[1024,512]{0,1:T(8,128)(2,1)}, bf16[1024,512]{0,1:T(8,128)(2,1)S(1)}, u32[]{:S(2)}) copy-start(bf16[1024,512]{0,1:T(8,128)(2,1)S(1)} %copy.76) | copy-start | bytes 3145732
  33.5 2.1 copy-start.10
  33.5 91.7 %copy-start.8 = (f32[512]{0:T(512)S(1)}, f32[512]{0:T(512)}, u32[]{:S(2)}) copy-start(f32[512]{0:T(512)} %param.16) | copy-start | bytes 6148
  200.9 4.7 %copy-start.5 = (bf16[8,1024,128]{2,0,1:T(8,128)(2,1)S(1)}, bf16[8,1024,128]{2,0,1:T(8,128)(2,1)}, u32[]{:S(2)}) copy-start(bf16[8,1024,128]{2,0,1:T(8,128)(2,1)} %convolution_convert_fusion.1) | copy-start | bytes 6291460
  205.6 1.8 copy-start.3
  212.0 1.0 copy-start.4
  216.0 104.6 %reduce-scatter.2.cloned.1.call-start = ((), (), s32[]{:S(2)}) async-start(), calls=%async_computation.4 | async-start | bytes 4456448 | tf_op jit(solution)/shard_map/reduce_scatter | solution.py:92
  227.2 0.8 copy-start.7
  227.2 0.8 copy-start.11
  260.4 2.1 copy-start.9
  260.4 2.2 copy-start.1
Sparse Core Ops, SparseCore 0:
  23.0 44.4 all-gather.5
  216.1 40.0 all-gather.7
  258.7 61.7 reduce-scatter.1
